TPU v7x, 32 devices: a whole 2x2x4 slice. The times are simulated.
32 devices in a mesh: row: 4 (over z), col: 4 (over x, core), ch: 2 (over y).
Axes of the slice: x: 2, y: 2, z: 4, core: 2. Of those that a mesh axis runs over, the one named last changes fastest.
Arguments:
- image_tokens: bfloat16 [64, 1024, 128], P(('row', 'ch'), 'col'), may hold values from -61 to 61
- labels: int32 [64, 1024], P(('row', 'ch'), 'col'), may hold values from 0 to 2
- rel_index: int32 [64, 64], replicated, may hold values from 0 to 224
- norm_gain: float32 [2, 2, 128], replicated, may hold values from 0.25 to 1.75
- norm_shift: float32 [2, 2, 128], replicated, may hold values from -1.5 to 1.5
- qkv_weight: bfloat16 [2, 3, 128, 128], P(None, None, None, 'ch'), may hold values from -5 to 5
- qkv_bias: float32 [2, 3, 128], P(None, None, 'ch'), may hold values from -1.5 to 1.5
- bias_table: float32 [2, 225, 4], P(None, None, 'ch'), may hold values from -4 to 4
- proj_weight: bfloat16 [2, 128, 128], P(None, 'ch'), may hold values from -0.5 to 0.5
- proj_bias: float32 [2, 128], replicated, may hold values from -1.5 to 1.5
- fc1_weight: bfloat16 [2, 128, 512], P(None, None, 'ch'), may hold values from -0.5 to 0.5
- fc1_bias: float32 [2, 512], P(None, 'ch'), may hold values from -2.5 to 2.5
- fc2_weight: bfloat16 [2, 512, 128], P(None, 'ch'), may hold values from -0.25 to 0.25
- fc2_bias: float32 [2, 128], replicated, may hold values from -1.5 to 1.5
Outputs:
- encoded: bfloat16 [64, 1024, 128], P(('row', 'ch'), 'col')
All inputs are finite; a program needn't handle non-finite values.
Results may differ from a plain program's by a relative error of at most 0.014.
Values may be sent and summed in bfloat16 or wider, within the bound.
A program may use at most 128 MiB of HBM per device.

v0:
```python
import functools
import math

import jax
import jax.numpy as jnp
from jax import lax
from jax.experimental import pallas as pl
from jax.experimental.pallas import tpu as pltpu
from jax.sharding import PartitionSpec as P

WIN = 8
SHIFT = 4
BLOCKS = 2
EPS = 1e-05
FAR = -1e30
CLASSES = 16
bf16 = jnp.bfloat16
f32 = jnp.float32


def padded(shard, sides, width):
    for axis, dim in sides:
        size, length = (lax.axis_size(axis), shard.shape[dim])
        up = [(i, (i + 1) % size) for i in range(size)]
        down = [(j, i) for i, j in up]
        last = lax.slice_in_dim(shard, length - width, length, axis=dim)
        leading = lax.slice_in_dim(shard, 0, width, axis=dim)
        before = lax.ppermute(last, axis, up)
        after = lax.ppermute(leading, axis, down)
        shard = jnp.concatenate([before, shard, after], axis=dim)
    return shard


def position_bias(rel_index, table):
    entries = table.shape[0]
    onehot = (rel_index.reshape(-1, 1) == jnp.arange(entries, dtype=jnp.int32)[None, :]).astype(f32)
    picked = jnp.dot(onehot, table, precision=lax.Precision.HIGHEST, preferred_element_type=f32)
    length = rel_index.shape[0]
    return picked.T.reshape(table.shape[1], length, length)


def dot(a, b):
    return jnp.dot(a, b, preferred_element_type=f32)


def dot_t(a, b):
    return lax.dot_general(a, b, (((1,), (1,)), ((), ())), preferred_element_type=f32)


def layer_norm(x, gain, offset):
    center = x - jnp.mean(x, axis=-1, keepdims=True)
    spread = jnp.mean(center * center, axis=-1, keepdims=True)
    return (center * lax.rsqrt(spread + EPS) * gain + offset).astype(bf16)


def rows_of(x):
    return x.reshape(x.shape[0] * x.shape[1], x.shape[2])


def attend(q, k, v, hmask, bias, heads, depth, far=None):
    keys = k.shape[0]
    kb = jnp.concatenate([k] * heads, axis=0) * hmask
    vb = jnp.concatenate([v] * heads, axis=0) * hmask
    if far is not None:
        fq, fk = far
        q = jnp.concatenate([q, fq], axis=1)
        kb = jnp.concatenate([kb, jnp.concatenate([fk] * heads, axis=0)], axis=1)
    s = dot_t(q, kb) * (depth ** (-0.5)) + bias
    per = 128 // keys
    parts = []
    lane = lax.broadcasted_iota(jnp.int32, (s.shape[0], 128), 1)
    for c in range(0, s.shape[1], 128):
        t = s[:, c : c + 128]
        top = None
        for j in range(per):
            inside = (lane >= j * keys) & (lane < (j + 1) * keys)
            peak = jnp.max(jnp.where(inside, t, -jnp.inf), axis=-1, keepdims=True)
            top = peak if top is None else jnp.where(lane >= j * keys, peak, top)
        parts.append(jnp.exp(t - top))
    p = jnp.concatenate(parts, axis=1).astype(bf16)
    o = dot(p, jnp.concatenate([vb, hmask], axis=1))
    width = q.shape[1] if far is None else k.shape[1]
    return (o[:, :width] / o[:, width:]).astype(bf16)


def finish(x, attended, w, b):
    mixed = dot(attended, w["proj"][b])
    middle = (x + mixed + w["proj_b"][b]).astype(bf16).astype(f32)
    normed = layer_norm(middle, w["gain"][b][1:2], w["shift"][b][1:2])
    inner = dot(normed, w["fc1"][b]) + w["fc1_b"][b]
    hidden = (0.5 * inner * (1.0 + lax.erf(inner * (0.5 ** 0.5)))).astype(bf16)
    outer = dot(hidden, w["fc2"][b])
    return (middle + outer + w["fc2_b"][b]).astype(bf16)


NAMES = ("gain", "shift", "qkv", "qkv_b", "bias", "proj", "proj_b", "fc1", "fc1_b", "fc2", "fc2_b")


def head_mask(heads, keys, width):
    depth = width // heads
    row = lax.broadcasted_iota(jnp.int32, (heads * keys, width), 0) // keys
    col = lax.broadcasted_iota(jnp.int32, (heads * keys, width), 1) // depth
    return (row == col).astype(f32).astype(bf16)


def qkv_of(x, w, b):
    normed = layer_norm(x, w["gain"][b][0:1], w["shift"][b][0:1])
    return dot(normed, w["qkv"][b]) + w["qkv_b"][b]


def first_chunk(x, w, heads, hmask):
    rows, wide, width = x.shape
    depth = width // heads
    toks = jnp.concatenate(
        [rows_of(x[:, c : c + WIN]) for c in range(0, wide, WIN)], axis=0
    )
    triple = qkv_of(toks, w, 0)
    outs = []
    n = WIN * WIN
    for g in range(wide // WIN):
        t = triple[g * n : (g + 1) * n].astype(bf16)
        outs.append(
            attend(t[:, :width], t[:, width : 2 * width], t[:, 2 * width :], hmask, w["bias"][0], heads, depth)
        )
    return finish(toks, jnp.concatenate(outs, axis=0), w, 0)


def kernel0(heads, chunk, x_ref, *refs):
    w = dict(zip(NAMES, refs[: len(NAMES)]))
    o_ref = refs[len(NAMES)]
    rows, cols, width = x_ref.shape
    hmask = head_mask(heads, WIN * WIN, width)

    def body(i, _):
        at = pl.ds(pl.multiple_of(i * chunk, chunk), chunk)
        y = first_chunk(x_ref[:, at, :].astype(f32), w, heads, hmask).astype(f32)
        n = WIN * WIN
        y = jnp.concatenate(
            [y[g * n : (g + 1) * n].reshape(WIN, WIN, width) for g in range(chunk // WIN)], axis=1
        )
        o_ref[:, at, :] = y.astype(bf16)
        return 0

    lax.fori_loop(0, cols // chunk, body, 0)


def second_chunk(x, fq, fk, w, heads, hmask):
    rows, wide, width = x.shape
    depth = width // heads
    half = WIN // 2
    outs, toks = [], []
    n = WIN * WIN
    for r in range(0, rows, WIN):
        xs = [rows_of(x[r : r + WIN, c : c + WIN]) for c in range(0, wide, WIN)]
        fqs = [rows_of(fq[r : r + WIN, c : c + WIN]) for c in range(0, wide, WIN)]
        fks = [rows_of(fk[r : r + WIN, c : c + WIN]) for c in range(0, wide, WIN)]
        triple = qkv_of(jnp.concatenate(xs, axis=0), w, 1)
        own = slice(half * WIN, n) if r == 0 else slice(0, half * WIN)
        bias = w["bias"][1][own, :]
        for g in range(wide // WIN):
            t = triple[g * n : (g + 1) * n].astype(bf16)
            outs.append(
                attend(
                    t[own, :width], t[:, width : 2 * width], t[:, 2 * width :], hmask, bias, heads, depth,
                    (fqs[g][own].astype(bf16), fks[g].astype(bf16)),
                )
            )
            toks.append(xs[g][own])
    return finish(jnp.concatenate(toks, axis=0), jnp.concatenate(outs, axis=0), w, 1)


def kernel1(heads, chunk, x_ref, reg_ref, *refs):
    w = dict(zip(NAMES, refs[: len(NAMES)]))
    o_ref, ext, fqr, fkr, res = refs[len(NAMES) :]
    rows, wide, width = x_ref.shape
    hmask = head_mask(heads, WIN * WIN, width)
    ext[...] = x_ref[...].astype(f32)
    lanes = reg_ref.shape[1]
    kinds = lax.broadcasted_iota(jnp.int32, (128, lanes), 0)
    for r in range(rows):
        same = (reg_ref[r : r + 1, :] == kinds).astype(f32).T[:wide]
        fqr[r] = same * FAR
        fkr[r] = 1.0 - same
    half = WIN // 2

    def body(i, _):
        at = pl.ds(pl.multiple_of(i * chunk, WIN), chunk)
        y = second_chunk(ext[:, at, :], fqr[:, at, :], fkr[:, at, :], w, heads, hmask).astype(f32)
        n = half * WIN
        g = chunk // WIN
        for r in range(2):
            for j in range(g):
                k = (r * g + j) * n
                col = pl.ds(pl.multiple_of(i * chunk + j * WIN, WIN), WIN)
                res[r * half : (r + 1) * half, col, :] = y[k : k + n].reshape(half, WIN, width)
        return 0

    lax.fori_loop(0, wide // chunk, body, 0)
    o_ref[...] = res[:, SHIFT : SHIFT + o_ref.shape[1], :].astype(bf16)


def chunk_of(windows, most):
    return max(d for d in range(1, most + 1) if windows % d == 0) * WIN


def on_device(
    image_tokens, labels, rel_index, norm_gain, norm_shift, qkv_weight, qkv_bias, bias_table,
    proj_weight, proj_bias, fc1_weight, fc1_bias, fc2_weight, fc2_bias,
):
    own_rows, tile_cols, width = image_tokens.shape
    groups = lax.axis_size("ch")
    first_row = (lax.axis_index("row") * groups + lax.axis_index("ch")) * own_rows
    image_rows = own_rows * groups * lax.axis_size("row")
    image_cols = tile_cols * lax.axis_size("col")
    margin = padded(labels, ((("row", "ch"), 0), ("col", 1)), SHIFT)
    grid_rows = jnp.mod(first_row - SHIFT + jnp.arange(own_rows + 2 * SHIFT, dtype=jnp.int32), image_rows)
    grid_cols = jnp.mod(
        lax.axis_index("col") * tile_cols - SHIFT + jnp.arange(tile_cols + 2 * SHIFT, dtype=jnp.int32), image_cols
    )
    region = (
        margin * 4
        + (grid_rows < SHIFT).astype(jnp.int32)[:, None] * 2
        + (grid_cols < SHIFT).astype(jnp.int32)[None, :]
    )
    region = jnp.pad(region, ((0, 0), (0, -region.shape[1] % 128)))
    qkv = lax.all_gather(qkv_weight, "ch", axis=3, tiled=True)
    proj = lax.all_gather(proj_weight, "ch", axis=1, tiled=True)
    fc1 = lax.all_gather(fc1_weight, "ch", axis=2, tiled=True)
    fc2 = lax.all_gather(fc2_weight, "ch", axis=1, tiled=True)
    qkv_b = lax.all_gather(qkv_bias, "ch", axis=2, tiled=True)
    table = lax.all_gather(bias_table, "ch", axis=2, tiled=True)
    fc1_b = lax.all_gather(fc1_bias, "ch", axis=1, tiled=True)
    heads = table.shape[2]
    n = WIN * WIN
    bias = jnp.stack([
        position_bias(rel_index, table[b]).transpose(1, 0, 2).reshape(n, heads * n) for b in range(BLOCKS)
    ])
    weights = (
        norm_gain, norm_shift,
        qkv.transpose(0, 2, 1, 3).reshape(BLOCKS, width, 3 * width), qkv_b.reshape(BLOCKS, 1, 3 * width),
        bias, proj, proj_bias[:, None], fc1, fc1_b[:, None], fc2, fc2_bias[:, None],
    )
    vmem = pl.BlockSpec(memory_space=pltpu.VMEM)
    params = pltpu.CompilerParams(vmem_limit_bytes=60 * 1024 * 1024)
    x1 = pl.pallas_call(
        functools.partial(kernel0, heads, chunk_of(tile_cols // WIN, 8)),
        out_shape=jax.ShapeDtypeStruct(image_tokens.shape, bf16),
        in_specs=[vmem] * (1 + len(weights)),
        out_specs=vmem,
        compiler_params=params,
        name="regular",
    )(image_tokens, *weights)
    ext = padded(x1, ((("row", "ch"), 0), ("col", 1)), SHIFT)
    return pl.pallas_call(
        functools.partial(kernel1, heads, chunk_of(tile_cols // WIN + 1, 11)),
        out_shape=jax.ShapeDtypeStruct(image_tokens.shape, bf16),
        in_specs=[vmem] * (2 + len(weights)),
        out_specs=vmem,
        scratch_shapes=[
            pltpu.VMEM(ext.shape, f32),
            pltpu.VMEM(ext.shape[:2] + (128,), f32),
            pltpu.VMEM(ext.shape[:2] + (128,), f32),
            pltpu.VMEM((own_rows,) + ext.shape[1:], f32),
        ],
        compiler_params=params,
        name="shifted",
    )(ext, region, *weights)


def solution(mesh):
    in_specs = (
        P(("row", "ch"), "col", None), P(("row", "ch"), "col"), P(), P(), P(),
        P(None, None, None, "ch"), P(None, None, "ch"), P(None, None, "ch"), P(None, "ch", None), P(),
        P(None, None, "ch"), P(None, "ch"), P(None, "ch", None), P(),
    )
    out_specs = P(("row", "ch"), "col", None)
    return jax.shard_map(on_device, mesh=mesh, in_specs=in_specs, out_specs=out_specs, check_vma=False)
```

profile of v0, /device:TPU:0, one launch (start us, length us, event | category | flops | bytes accessed | tf_op | source)
XLA Modules:
  0.0 99.6 jit_solution(8886477943118385943)
XLA Ops:
  0.0 0.7 copy.28
  0.7 5.3 %all_gather.23 = f32[2,225,4]{1,0,2:T(2,128)S(1)} all-gather(f32[2,225,2]{1,0,2:T(2,128)S(1)} %copy.28), channel_id=1, replica_groups=mesh['row'=4,'col'=4,'ch'=2] {'ch'}, dimensions={2}, use_global_device_ids=true | all-gather | bytes 10800 | tf_op jit(solution)/shard_map/all_gather | solution.py:231
  6.0 0.8 eq.12
  6.8 2.2 %convolution_bitcast_fusion.1 = f32[4,4096]{1,0:T(4,128)S(1)} fusion(s32[4096]{0:T(1024)S(1)} %eq.12, f32[1,225,4]{1,0,2:T(1,128)S(1)} %get-tuple-element.14), kind=kOutput, calls=%fused_computation.1 | convolution fusion | flops 45158400 | bytes 85520 | tf_op jit(solution)/shard_map/dot_general | solution.py:37
  9.0 0.1 reshape.52
  9.3 0.1 stack_reshape.6
  9.4 2.2 %convolution_bitcast_fusion = f32[4,4096]{1,0:T(4,128)S(1)} fusion(s32[4096]{0:T(1024)S(1)} %eq.12, f32[1,225,4]{1,0,2:T(1,128)S(1)} %get-tuple-element.13), kind=kOutput, calls=%fused_computation | convolution fusion | flops 45158400 | bytes 85520 | tf_op jit(solution)/shard_map/dot_general | solution.py:37
  11.6 0.1 reshape.53
  11.9 0.1 stack_reshape.7
  12.0 5.3 %all_gather.21 = bf16[2,3,128,128]{2,3,1,0:T(8,128)(2,1)S(1)} all-gather(bf16[2,3,128,64]{2,3,1,0:T(8,128)(2,1)S(1)} %copy-done.4), channel_id=1, replica_groups=mesh['row'=4,'col'=4,'ch'=2] {'ch'}, dimensions={3}, use_global_device_ids=true | all-gather | bytes 294912 | tf_op jit(solution)/shard_map/all_gather | solution.py:226
  17.3 0.8 copy.31.refs_2_
  18.1 5.7 %all_gather.25.refs_7_ = bf16[2,128,512]{2,1,0:T(8,128)(2,1)} all-gather(bf16[2,128,256]{2,1,0:T(8,128)(2,1)S(1)} %copy-done.2), channel_id=1, replica_groups=mesh['row'=4,'col'=4,'ch'=2] {'ch'}, dimensions={2}, use_global_device_ids=true | all-gather | bytes 393216 | tf_op jit(solution)/shard_map/all_gather | solution.py:228
  23.9 6.7 %all_gather.27.refs_9_ = bf16[2,512,128]{2,1,0:T(8,128)(2,1)} all-gather(bf16[2,256,128]{2,1,0:T(8,128)(2,1)S(1)} %copy-done.3), channel_id=1, replica_groups=mesh['row'=4,'col'=4,'ch'=2] {'ch'}, dimensions={1}, use_global_device_ids=true | all-gather | bytes 393216 | tf_op jit(solution)/shard_map/all_gather | solution.py:229
  30.6 0.1 copy.26
  30.7 4.9 %all_gather.22 = f32[2,3,128]{1,0,2:T(2,128)S(1)} all-gather(f32[2,3,64]{1,0,2:T(2,128)S(1)} %copy.26), channel_id=1, replica_groups=mesh['row'=4,'col'=4,'ch'=2] {'ch'}, dimensions={2}, use_global_device_ids=true | all-gather | bytes 4608 | tf_op jit(solution)/shard_map/all_gather | solution.py:230
  35.7 0.6 reshape.54.refs_3_
  36.3 4.7 %all_gather.24.refs_5_ = bf16[2,128,128]{2,1,0:T(8,128)(2,1)} all-gather(bf16[2,64,128]{2,1,0:T(8,128)(2,1)S(1)} %copy-done.6), channel_id=1, replica_groups=mesh['row'=4,'col'=4,'ch'=2] {'ch'}, dimensions={1}, use_global_device_ids=true | all-gather | bytes 98304 | tf_op jit(solution)/shard_map/all_gather | solution.py:227
  41.0 4.4 %all_gather.26 = f32[2,512]{1,0:T(2,128)S(1)} all-gather(f32[2,256]{1,0:T(2,128)S(1)} %copy-done.8), channel_id=1, replica_groups=mesh['row'=4,'col'=4,'ch'=2] {'ch'}, dimensions={1}, use_global_device_ids=true | all-gather | bytes 6144 | tf_op jit(solution)/shard_map/all_gather | solution.py:232
  45.3 0.6 broadcast_in_dim.14.refs_8_
  45.9 0.6 copy-done.1
  46.6 8.7 %regular.1 = bf16[8,256,128]{2,1,0:T(8,128)(2,1)} custom-call(bf16[8,256,128]{2,1,0:T(8,128)(2,1)} %x_ref.1, f32[2,2,128]{2,1,0:T(2,128)} %refs_0_.3, f32[2,2,128]{2,1,0:T(2,128)} %refs_1_.3, bf16[2,128,384]{2,1,0:T(8,128)(2,1)} %copy.31.refs_2_, f32[2,1,384]{2,1,0:T(1,128)} %reshape.54.refs_3_, f32[2,64,256]{2,1,0:T(8,128)} %copy-done.1, ...), custom_call_target="tpu_custom_call" | custom-call | tf_op jit(solution)/shard_map/regular/pallas_call | solution.py:245
  55.3 1.1 %fusion.12 = (bf16[4,256,128]{2,1,0:T(8,128)(2,1)S(1)}, bf16[4,256,128]{2,1,0:T(8,128)(2,1)S(1)}) fusion(bf16[8,256,128]{2,1,0:T(8,128)(2,1)} %regular.1), kind=kLoop, calls=%fused_computation.32 | loop fusion | bytes 1048576 | tf_op jit(solution)/shard_map/slice | solution.py:26
  56.4 2.1 %collective-permute-start = (bf16[4,256,128]{2,1,0:T(8,128)(2,1)S(1)}, bf16[4,256,128]{2,1,0:T(8,128)(2,1)S(1)}, u32[]{:S(2)}, u32[]{:S(2)}) collective-permute-start(bf16[4,256,128]{2,1,0:T(8,128)(2,1)S(1)} %get-tuple-element.7), channel_id=1, source_target_pairs={{0,1},{1,8},{8,9},{9,16},{16,17},{17,24},{24,25},{25,0},{2,3},{3,1... | collective-permute-start | bytes 786440 | tf_op jit(solution)/shard_map/ppermute | solution.py:28
  58.5 3.1 %collective-permute-start.1 = (bf16[4,256,128]{2,1,0:T(8,128)(2,1)S(1)}, bf16[4,256,128]{2,1,0:T(8,128)(2,1)S(1)}, u32[]{:S(2)}, u32[]{:S(2)}) collective-permute-start(bf16[4,256,128]{2,1,0:T(8,128)(2,1)S(1)} %get-tuple-element.8), channel_id=1, source_target_pairs={{1,0},{8,1},{9,8},{16,9},{17,16},{24,17},{25,24},{0,25},{3,2},{10,... | collective-permute-start | bytes 786440 | tf_op jit(solution)/shard_map/ppermute | solution.py:29
  61.6 4.7 %collective-permute-start.5 = (s32[4,256]{1,0:T(4,128)S(1)}, s32[4,256]{1,0:T(4,128)S(1)}, u32[]{:S(2)}, u32[]{:S(2)}) collective-permute-start(s32[4,256]{1,0:T(4,128)S(1)} %get-tuple-element.12), channel_id=1, source_target_pairs={{1,0},{8,1},{9,8},{16,9},{17,16},{24,17},{25,24},{0,25},{3,2},{10,... | collective-permute-start | bytes 12296 | tf_op jit(solution)/shard_map/ppermute | solution.py:29
  66.4 1.6 %collective-permute-done.4 = s32[4,256]{1,0:T(4,128)S(1)} collective-permute-done((s32[4,256]{1,0:T(4,128)S(1)}, s32[4,256]{1,0:T(4,128)S(1)}, u32[]{:S(2)}, u32[]{:S(2)}) %collective-permute-start.4) | collective-permute-done | bytes 4128 | tf_op jit(solution)/shard_map/ppermute | solution.py:28
  68.0 1.7 %collective-permute-start.7 = (s32[16,4]{1,0:T(8,128)S(1)}, s32[16,4]{1,0:T(8,128)S(1)}, u32[]{:S(2)}, u32[]{:S(2)}) collective-permute-start(s32[16,4]{1,0:T(8,128)S(1)} %get-tuple-element.10), channel_id=1, source_target_pairs={{2,0},{4,2},{6,4},{0,6},{3,1},{5,3},{7,5},{1,7},{10,8},{12,10},{14... | collective-permute-start | bytes 776 | tf_op jit(solution)/shard_map/ppermute | solution.py:29
  69.9 1.7 %collective-permute-start.3 = (bf16[16,4,128]{2,1,0:T(4,128)(2,1)S(1)}, bf16[16,4,128]{2,1,0:T(4,128)(2,1)S(1)}, u32[]{:S(2)}, u32[]{:S(2)}) collective-permute-start(bf16[16,4,128]{2,1,0:T(4,128)(2,1)S(1)} %get-tuple-element.6), channel_id=1, source_target_pairs={{2,0},{4,2},{6,4},{0,6},{3,1},{5,3},{7,5},{1,7},{10,8},{12,10},{14... | collective-permute-start | bytes 49160 | tf_op jit(solution)/shard_map/ppermute | solution.py:29
  71.7 0.6 pad.4.reg_ref
  72.3 0.8 collective-permute-done.2
  73.1 1.3 %pad_maximum_fusion.x_ref = bf16[16,264,128]{2,1,0:T(8,128)(2,1)} fusion(bf16[16,4,128]{2,1,0:T(4,128)(2,1)S(1)} %collective-permute-done.3, bf16[4,256,128]{2,1,0:T(8,128)(2,1)S(1)} %collective-permute-done.1, bf16[8,256,128]{2,1,0:T(8,128)(2,1)S(1)} %copy-done, bf16[4,256,128]{2,1,0:T(8,128)(2,1)S(1)} %collective-permute-done, ...), kind=kLoop, calls=%fused_computation.5 | loop fusion | flops 5406720 | bytes 2162688 | tf_op jit(solution)/shard_map/concatenate | solution.py:30
  74.4 25.2 %shifted.1 = bf16[8,256,128]{2,1,0:T(8,128)(2,1)} custom-call(bf16[16,264,128]{2,1,0:T(8,128)(2,1)} %pad_maximum_fusion.x_ref, s32[16,384]{1,0:T(8,128)} %pad.4.reg_ref, f32[2,2,128]{2,1,0:T(2,128)} %refs_0_.3, f32[2,2,128]{2,1,0:T(2,128)} %refs_1_.3, bf16[2,128,384]{2,1,0:T(8,128)(2,1)} %copy.31.refs_2_, f32[2,1,384]{2,1,0:T(1,128)} %reshape.54.refs_3_, ...), custom_call_target="tpu_custom_call" | custom-call | tf_op jit(solution)/shard_map/shifted/pallas_call | solution.py:254
  (39 shorter events, 0.6 us)
Async XLA Ops:
  9.2 2.8 %copy-start.4 = (bf16[2,3,128,64]{2,3,1,0:T(8,128)(2,1)S(1)}, bf16[2,3,128,64]{2,3,1,0:T(8,128)(2,1)}, u32[]{:S(2)}) copy-start(bf16[2,3,128,64]{2,3,1,0:T(8,128)(2,1)} %param.19) | copy-start | bytes 294916
  9.4 8.7 %copy-start.2 = (bf16[2,128,256]{2,1,0:T(8,128)(2,1)S(1)}, bf16[2,128,256]{2,1,0:T(8,128)(2,1)}, u32[]{:S(2)}) copy-start(bf16[2,128,256]{2,1,0:T(8,128)(2,1)} %param.24) | copy-start | bytes 393220
  11.6 12.2 %copy-start.3 = (bf16[2,256,128]{2,1,0:T(8,128)(2,1)S(1)}, bf16[2,256,128]{2,1,0:T(8,128)(2,1)}, u32[]{:S(2)}) copy-start(bf16[2,256,128]{2,1,0:T(8,128)(2,1)} %param.26) | copy-start | bytes 393220
  11.6 18.9 %copy-start.7 = (f32[2,3,64]{2,0,1:T(2,128)S(1)}, f32[2,3,64]{2,0,1:T(2,128)}, u32[]{:S(2)}) copy-start(f32[2,3,64]{2,0,1:T(2,128)} %param.20) | copy-start | bytes 4612
  11.9 24.4 %copy-start.6 = (bf16[2,64,128]{2,1,0:T(8,128)(2,1)S(1)}, bf16[2,64,128]{2,1,0:T(8,128)(2,1)}, u32[]{:S(2)}) copy-start(bf16[2,64,128]{2,1,0:T(8,128)(2,1)} %param.22) | copy-start | bytes 98308
  11.9 29.1 %copy-start.8 = (f32[2,256]{1,0:T(2,128)S(1)}, f32[2,256]{1,0:T(2,128)}, u32[]{:S(2)}) copy-start(f32[2,256]{1,0:T(2,128)} %param.25) | copy-start | bytes 6148
  45.9 0.6 copy-start.1
  46.6 15.0 %copy-start.5 = (s32[8,256]{1,0:T(8,128)S(1)}, s32[8,256]{1,0:T(8,128)}, u32[]{:S(2)}) copy-start(s32[8,256]{1,0:T(8,128)} %param.15) | copy-start | bytes 24580
  55.3 14.5 %copy-start = (bf16[8,256,128]{2,1,0:T(8,128)(2,1)S(1)}, bf16[8,256,128]{2,1,0:T(8,128)(2,1)}, u32[]{:S(2)}) copy-start(bf16[8,256,128]{2,1,0:T(8,128)(2,1)} %regular.1) | copy-start | bytes 1572868
  56.4 13.3 %collective-permute-start = (bf16[4,256,128]{2,1,0:T(8,128)(2,1)S(1)}, bf16[4,256,128]{2,1,0:T(8,128)(2,1)S(1)}, u32[]{:S(2)}, u32[]{:S(2)}) collective-permute-start(bf16[4,256,128]{2,1,0:T(8,128)(2,1)S(1)} %get-tuple-element.7), channel_id=1, source_target_pairs={{0,1},{1,8},{8,9},{9,16},{16,17},{17,24},{24,25},{25,0},{2,3},{3,1... | collective-permute-start | bytes 786440 | tf_op jit(solution)/shard_map/ppermute | solution.py:28
  58.5 11.3 %collective-permute-start.1 = (bf16[4,256,128]{2,1,0:T(8,128)(2,1)S(1)}, bf16[4,256,128]{2,1,0:T(8,128)(2,1)S(1)}, u32[]{:S(2)}, u32[]{:S(2)}) collective-permute-start(bf16[4,256,128]{2,1,0:T(8,128)(2,1)S(1)} %get-tuple-element.8), channel_id=1, source_target_pairs={{1,0},{8,1},{9,8},{16,9},{17,16},{24,17},{25,24},{0,25},{3,2},{10,... | collective-permute-start | bytes 786440 | tf_op jit(solution)/shard_map/ppermute | solution.py:29
  61.6 6.3 %collective-permute-start.4 = (s32[4,256]{1,0:T(4,128)S(1)}, s32[4,256]{1,0:T(4,128)S(1)}, u32[]{:S(2)}, u32[]{:S(2)}) collective-permute-start(s32[4,256]{1,0:T(4,128)S(1)} %get-tuple-element.11), channel_id=1, source_target_pairs={{0,1},{1,8},{8,9},{9,16},{16,17},{17,24},{24,25},{25,0},{2,3},{3,1... | collective-permute-start | bytes 12296 | tf_op jit(solution)/shard_map/ppermute | solution.py:28
  61.6 6.3 %collective-permute-start.5 = (s32[4,256]{1,0:T(4,128)S(1)}, s32[4,256]{1,0:T(4,128)S(1)}, u32[]{:S(2)}, u32[]{:S(2)}) collective-permute-start(s32[4,256]{1,0:T(4,128)S(1)} %get-tuple-element.12), channel_id=1, source_target_pairs={{1,0},{8,1},{9,8},{16,9},{17,16},{24,17},{25,24},{0,25},{3,2},{10,... | collective-permute-start | bytes 12296 | tf_op jit(solution)/shard_map/ppermute | solution.py:29
  68.0 3.6 %collective-permute-start.6 = (s32[16,4]{1,0:T(8,128)S(1)}, s32[16,4]{1,0:T(8,128)S(1)}, u32[]{:S(2)}, u32[]{:S(2)}) collective-permute-start(s32[16,4]{1,0:T(8,128)S(1)} %get-tuple-element.9), channel_id=1, source_target_pairs={{0,2},{2,4},{4,6},{6,0},{1,3},{3,5},{5,7},{7,1},{8,10},{10,12},{12... | collective-permute-start | bytes 776 | tf_op jit(solution)/shard_map/ppermute | solution.py:28
  68.0 3.6 %collective-permute-start.7 = (s32[16,4]{1,0:T(8,128)S(1)}, s32[16,4]{1,0:T(8,128)S(1)}, u32[]{:S(2)}, u32[]{:S(2)}) collective-permute-start(s32[16,4]{1,0:T(8,128)S(1)} %get-tuple-element.10), channel_id=1, source_target_pairs={{2,0},{4,2},{6,4},{0,6},{3,1},{5,3},{7,5},{1,7},{10,8},{12,10},{14... | collective-permute-start | bytes 776 | tf_op jit(solution)/shard_map/ppermute | solution.py:29
  69.8 3.3 %collective-permute-start.2 = (bf16[16,4,128]{2,1,0:T(4,128)(2,1)S(1)}, bf16[16,4,128]{2,1,0:T(4,128)(2,1)S(1)}, u32[]{:S(2)}, u32[]{:S(2)}) collective-permute-start(bf16[16,4,128]{2,1,0:T(4,128)(2,1)S(1)} %get-tuple-element.5), channel_id=1, source_target_pairs={{0,2},{2,4},{4,6},{6,0},{1,3},{3,5},{5,7},{7,1},{8,10},{10,12},{12... | collective-permute-start | bytes 49160 | tf_op jit(solution)/shard_map/ppermute | solution.py:28
  69.9 3.2 %collective-permute-start.3 = (bf16[16,4,128]{2,1,0:T(4,128)(2,1)S(1)}, bf16[16,4,128]{2,1,0:T(4,128)(2,1)S(1)}, u32[]{:S(2)}, u32[]{:S(2)}) collective-permute-start(bf16[16,4,128]{2,1,0:T(4,128)(2,1)S(1)} %get-tuple-element.6), channel_id=1, source_target_pairs={{2,0},{4,2},{6,4},{0,6},{3,1},{5,3},{7,5},{1,7},{10,8},{12,10},{14... | collective-permute-start | bytes 49160 | tf_op jit(solution)/shard_map/ppermute | solution.py:29
where the time goes:
time: 101 us; the launch traced here: 99.6 us
  blocking collectives  37 us (37%)
  Pallas kernels  33.9 us (34%)
  starting transfers between devices  13.4 us (13%)
  local copies, waits for them, and re-layouts  6.94 us (7%)
  matrix products  4.38 us (4%)
  waiting for transfers between devices  2.37 us (2%)
  other arithmetic  1.45 us (1%)
    pallas_call x1, Pallas kernels, on_device(): pl.pallas_call(functools.partial(kernel1, heads, chunk_of(tile_cols // WI...  25.2 us
    ppermute x4, starting transfers between devices, padded(): after = lax.ppermute(leading, axis, down)  11.3 us
    pallas_call x1, Pallas kernels, on_device(): pl.pallas_call(functools.partial(kernel0, heads, chunk_of(tile_cols // WI...  8.69 us
    all_gather x1, blocking collectives, on_device(): fc2 = lax.all_gather(fc2_weight, 'ch', axis=1, tiled=True)  6.7 us
    all_gather x1, blocking collectives, on_device(): fc1 = lax.all_gather(fc1_weight, 'ch', axis=2, tiled=True)  5.73 us
    all_gather x1, blocking collectives, on_device(): table = lax.all_gather(bias_table, 'ch', axis=2, tiled=True)  5.3 us
    all_gather x1, blocking collectives, on_device(): qkv = lax.all_gather(qkv_weight, 'ch', axis=3, tiled=True)  5.29 us
    all_gather x1, blocking collectives, on_device(): qkv_b = lax.all_gather(qkv_bias, 'ch', axis=2, tiled=True)  4.93 us
  transfers between devices with their start and end apart: 8, of which 2 were waited for; matrix products, arithmetic and copies ran while one was open for 1% of the time, Pallas kernels for 0%

commit v1 on v0

v1 whole, which is shorter than its diff:
```python
import functools

import jax
import jax.numpy as jnp
from jax import lax
from jax.experimental import pallas as pl
from jax.experimental.pallas import tpu as pltpu
from jax.sharding import PartitionSpec as P

WIN = 8
SHIFT = 4
BLOCKS = 2
EPS = 1e-05
FAR = -1e30
bf16 = jnp.bfloat16
f32 = jnp.float32


def dot(a, b):
    return jnp.dot(a, b, preferred_element_type=f32)


def dot_t(a, b):
    return lax.dot_general(a, b, (((1,), (1,)), ((), ())), preferred_element_type=f32)


def layer_norm(x, gain, offset):
    center = x - jnp.mean(x, axis=-1, keepdims=True)
    spread = jnp.mean(center * center, axis=-1, keepdims=True)
    return (center * lax.rsqrt(spread + EPS) * gain + offset).astype(bf16)


def rows_of(x):
    return x.reshape(x.shape[0] * x.shape[1], x.shape[2])


def attend(q, k, v, hmask, bias, heads, depth, far=None):
    keys = k.shape[0]
    kb = jnp.concatenate([k] * heads, axis=0) * hmask
    vb = jnp.concatenate([v] * heads, axis=0) * hmask
    if far is not None:
        fq, fk = far
        q = jnp.concatenate([q, fq], axis=1)
        kb = jnp.concatenate([kb, jnp.concatenate([fk] * heads, axis=0)], axis=1)
    s = dot_t(q, kb) * (depth ** (-0.5)) + bias
    per = 128 // keys
    parts = []
    lane = lax.broadcasted_iota(jnp.int32, (s.shape[0], 128), 1)
    for c in range(0, s.shape[1], 128):
        t = s[:, c : c + 128]
        top = None
        for j in range(per):
            inside = (lane >= j * keys) & (lane < (j + 1) * keys)
            peak = jnp.max(jnp.where(inside, t, -jnp.inf), axis=-1, keepdims=True)
            top = peak if top is None else jnp.where(lane >= j * keys, peak, top)
        parts.append(jnp.exp(t - top))
    p = jnp.concatenate(parts, axis=1).astype(bf16)
    o = dot(p, jnp.concatenate([vb, hmask], axis=1))
    width = q.shape[1] if far is None else k.shape[1]
    return (o[:, :width] / o[:, width:]).astype(bf16)


def finish(x, attended, w, b):
    mixed = dot(attended, w["proj"][b])
    middle = (x + mixed + w["proj_b"][b]).astype(bf16).astype(f32)
    normed = layer_norm(middle, w["gain"][b][1:2], w["shift"][b][1:2])
    inner = dot(normed, w["fc1"][b]) + w["fc1_b"][b]
    hidden = (0.5 * inner * (1.0 + lax.erf(inner * (0.5 ** 0.5)))).astype(bf16)
    outer = dot(hidden, w["fc2"][b])
    return (middle + outer + w["fc2_b"][b]).astype(bf16)


def head_mask(heads, keys, width):
    depth = width // heads
    row = lax.broadcasted_iota(jnp.int32, (heads * keys, width), 0) // keys
    col = lax.broadcasted_iota(jnp.int32, (heads * keys, width), 1) // depth
    return (row == col).astype(f32).astype(bf16)


def qkv_of(x, w, b):
    normed = layer_norm(x, w["gain"][b][0:1], w["shift"][b][0:1])
    return dot(normed, w["qkv"][b]) + w["qkv_b"][b]


def first_chunk(x, w, heads, hmask):
    rows, wide, width = x.shape
    depth = width // heads
    toks = jnp.concatenate(
        [rows_of(x[:, c : c + WIN]) for c in range(0, wide, WIN)], axis=0
    )
    triple = qkv_of(toks, w, 0)
    outs = []
    n = WIN * WIN
    for g in range(wide // WIN):
        t = triple[g * n : (g + 1) * n].astype(bf16)
        outs.append(
            attend(t[:, :width], t[:, width : 2 * width], t[:, 2 * width :], hmask, w["bias"][0], heads, depth)
        )
    return finish(toks, jnp.concatenate(outs, axis=0), w, 0)


def second_chunk(x, reg, w, heads, hmask):
    kinds = lax.broadcasted_iota(jnp.int32, (WIN * WIN, 128), 1).astype(f32)
    rows, wide, width = x.shape
    depth = width // heads
    half = WIN // 2
    outs, toks = [], []
    n = WIN * WIN
    for r in range(0, rows, WIN):
        xs = [rows_of(x[r : r + WIN, c : c + WIN]) for c in range(0, wide, WIN)]
        same = [(rows_of(reg[r : r + WIN, c : c + WIN]) == kinds).astype(f32) for c in range(0, wide, WIN)]
        triple = qkv_of(jnp.concatenate(xs, axis=0), w, 1)
        own = slice(half * WIN, n) if r == 0 else slice(0, half * WIN)
        bias = w["bias"][1][own, :]
        for g in range(wide // WIN):
            t = triple[g * n : (g + 1) * n].astype(bf16)
            outs.append(
                attend(
                    t[own, :width], t[:, width : 2 * width], t[:, 2 * width :], hmask, bias, heads, depth,
                    ((same[g][own] * FAR).astype(bf16), (1.0 - same[g]).astype(bf16)),
                )
            )
            toks.append(xs[g][own])
    return finish(jnp.concatenate(toks, axis=0), jnp.concatenate(outs, axis=0), w, 1)


def fused(
    heads, chunk0, chunk1,
    x_ref, lab_ref, rel_ref, gain, shift, qkv_w, qkv_b, table, proj_w, proj_b, fc1_w, fc1_b, fc2_w, fc2_b,
    o_ref,
    ext, regb, res, x1, top, bot, side, corner, lab, tsc, tab_own, tab_all,
    qkv_all, qb_all, f1b_all, qkv, qb, bias, proj, fc1, f1b, fc2,
    wsend, wrecv, rsend, rrecv, lsend, lrecv, hsend, hrecv, esend, erecv, own_sem,
):
    rows, cols, width = x_ref.shape
    n = lax.axis_size("ch")
    nrow, ncol = lax.axis_size("row"), lax.axis_size("col")
    row, col, ch = lax.axis_index("row"), lax.axis_index("col"), lax.axis_index("ch")
    ring = row * n + ch
    total = nrow * n

    def at(dr, dc):
        p = lax.rem(ring + dr + total, total)
        return (p // n, lax.rem(col + dc + ncol, ncol), lax.rem(p, n))

    around = [(-1, -1), (-1, 0), (-1, 1), (0, -1), (0, 1), (1, -1), (1, 0), (1, 1)]
    peers = [(row, col, lax.rem(ch + d, n)) for d in range(1, n)]
    mate = (row, col + 1 - 2 * lax.rem(col, 2), ch)
    core = lax.rem(col, 2)
    mesh_id = pl.DeviceIdType.MESH

    barrier = pltpu.get_barrier_semaphore()
    targets = [at(*d) for d in around] + peers + [mate]
    for t in targets:
        pl.semaphore_signal(barrier, inc=1, device_id=t, device_id_type=mesh_id)

    def remote(src, dst, ssem, rsem, to):
        return pltpu.make_async_remote_copy(
            src_ref=src, dst_ref=dst, send_sem=ssem, recv_sem=rsem, device_id=to, device_id_type=mesh_id
        )

    for b in range(BLOCKS):
        tsc[...] = jnp.zeros_like(tsc)
        tsc[: table.shape[1], : table.shape[2]] = table[b]
        tab_own[b] = tsc[...].T[:8]
    pl.semaphore_wait(barrier, len(targets))

    kh, ph, fh, gh = width // 2, proj_w.shape[1] // 2, width // 2, fc2_w.shape[1] // 2
    pw, fw, gw = proj_w.shape[1], fc1_w.shape[2], fc2_w.shape[1]

    def pieces(b, owner):
        k0, p0, f0, g0 = (pl.multiple_of(core * v, 16) for v in (kh, ph, fh, gh))
        return [
            (qkv_w.at[b, :, pl.ds(k0, kh), :], qkv_all.at[owner, b, :, pl.ds(k0, kh), :]),
            (proj_w.at[b, pl.ds(p0, ph), :], proj.at[b, pl.ds(pl.multiple_of(owner * pw + p0, 16), ph), :]),
            (
                fc1_w.at[b, pl.ds(f0, fh), :],
                fc1.at[b, pl.ds(f0, fh), pl.ds(pl.multiple_of(owner * fw, 128), fw)],
            ),
            (fc2_w.at[b, pl.ds(g0, gh), :], fc2.at[b, pl.ds(pl.multiple_of(owner * gw + g0, 16), gh), :]),
        ]

    direct, relays, smalls = {}, {}, []
    for d in range(1, n):
        to, owner = peers[d - 1], lax.rem(ch - d + n, n)
        for b in range(BLOCKS):
            for i, (src, dst) in enumerate(pieces(b, ch)):
                direct[d, b, i] = remote(src, dst, wsend.at[d - 1, b, i], wrecv.at[d - 1, b, i], to)
            for i, (_, dst) in enumerate(pieces(b, owner)):
                relays[d, b, i] = remote(dst, dst, rsend.at[d - 1, b, i], rrecv.at[d - 1, b, i], mate)
        for i, (src, dst) in enumerate(
            [(tab_own, tab_all.at[ch]), (qkv_b, qb_all.at[ch]), (fc1_b, f1b_all.at[ch])]
        ):
            smalls.append(remote(src, dst, wsend.at[d - 1, BLOCKS, i], wrecv.at[d - 1, BLOCKS, i], to))
    for c in smalls:
        c.start()
    for b in range(BLOCKS):
        for d in range(1, n):
            for i in range(4):
                direct[d, b, i].start()
    labels = []
    for i, d in enumerate(around):
        labels.append(remote(lab_ref, lab.at[i], lsend.at[i], lrecv.at[i], at(-d[0], -d[1])))
        labels[-1].start()
    locals_ = [
        (qkv_w, qkv_all.at[ch]),
        (proj_w, proj.at[:, pl.ds(pl.multiple_of(ch * pw, 16), pw), :]),
        (fc1_w, fc1.at[:, :, pl.ds(pl.multiple_of(ch * fw, 128), fw)]),
        (fc2_w, fc2.at[:, pl.ds(pl.multiple_of(ch * gw, 16), gw), :]),
        (tab_own, tab_all.at[ch]), (qkv_b, qb_all.at[ch]), (fc1_b, f1b_all.at[ch]),
    ]
    locals_ = [pltpu.make_async_copy(s, d, own_sem.at[i]) for i, (s, d) in enumerate(locals_)]
    for c in locals_:
        c.start()
    for c in locals_:
        c.wait()
    for c in smalls:
        c.wait()

    part = width // n
    keys = WIN * WIN
    for j in range(n):
        for b in range(BLOCKS):
            for m in range(3):
                qb[b, :, m * width + j * part : m * width + (j + 1) * part] = qb_all[j, b, m : m + 1, :]
            f1b[b, :, j * fw : (j + 1) * fw] = f1b_all[j, b : b + 1, :]
    local_heads = table.shape[2]
    per = 128 // keys
    idx = jnp.concatenate([rel_ref[...]] * per, axis=1)
    lane = lax.broadcasted_iota(jnp.int32, idx.shape, 1)
    for b in range(BLOCKS):
        for t in range(heads // per):
            out = None
            for j in range(per):
                h = t * per + j
                entry = tab_all[h // local_heads, b, h % local_heads : h % local_heads + 1, :]
                got = None
                for c in range(0, entry.shape[1], 128):
                    piece = jnp.broadcast_to(entry[:, c : c + 128], idx.shape)
                    here = jnp.take_along_axis(piece, idx & 127, axis=1, mode="promise_in_bounds")
                    got = here if got is None else jnp.where(idx >= c, here, got)
                out = got if out is None else jnp.where(lane >= j * keys, got, out)
            bias[b, :, t * 128 : (t + 1) * 128] = out

    def bring(b):
        for d in range(1, n):
            for i in range(4):
                direct[d, b, i].wait_recv()
                relays[d, b, i].start()

    def settle(b):
        for d in range(1, n):
            for i in range(4):
                relays[d, b, i].wait_recv()
        for j in range(n):
            for m in range(3):
                qkv[b, :, m * width + j * part : m * width + (j + 1) * part] = qkv_all[j, b, m]

    for c in labels:
        c.wait()
    def column(up, mid, down):
        return jnp.concatenate([up[rows - SHIFT :], mid, down[:SHIFT]], axis=0)
    west = column(lab[0], lab[3], lab[5]).astype(f32)
    mid = column(lab[1], lab_ref[...], lab[6]).astype(f32)
    east = column(lab[2], lab[4], lab[7]).astype(f32)
    tall = rows + 2 * SHIFT
    moved = pltpu.roll(jnp.concatenate([mid, jnp.zeros((tall, 128), f32)], axis=1), SHIFT, 1)
    span = cols + 128
    j = lax.broadcasted_iota(jnp.int32, (tall, span), 1)
    i = lax.broadcasted_iota(jnp.int32, (tall, span), 0)
    blank = jnp.zeros((tall, span - 128), f32)
    left = jnp.concatenate([pltpu.roll(west[:, cols - 128 :], SHIFT, 1), blank], axis=1)
    right = jnp.concatenate([blank, pltpu.roll(east[:, :128], SHIFT, 1)], axis=1)
    kind = jnp.where(j < SHIFT, left, jnp.where(j < cols + SHIFT, moved, right))
    def flag(here, when):
        return jnp.where(here, when.astype(f32), 0.0)
    low = flag((i >= SHIFT) & (i < 2 * SHIFT), ring == 0) + flag(i >= rows + SHIFT, ring == total - 1)
    front = flag((j >= SHIFT) & (j < 2 * SHIFT), col == 0) + flag(j >= cols + SHIFT, col == ncol - 1)
    kind = kind * 4.0 + low * 2.0 + front
    turned = kind.T[: cols + 2 * SHIFT].astype(bf16)
    pick = lax.broadcasted_iota(jnp.int32, (tall, 128), 0)
    for r in range(tall):
        regb[r] = dot(turned, (pick == r).astype(f32).astype(bf16))

    bring(0)
    bring(1)
    settle(0)

    w = {
        "gain": gain, "shift": shift, "qkv": qkv, "qkv_b": qb, "bias": bias, "proj": proj,
        "proj_b": [proj_b[b : b + 1] for b in range(BLOCKS)], "fc1": fc1, "fc1_b": f1b, "fc2": fc2,
        "fc2_b": [fc2_b[b : b + 1] for b in range(BLOCKS)],
    }
    hmask = head_mask(heads, keys, width)

    def halo(k):
        span = pl.ds(pl.multiple_of(k * chunk0, chunk0), chunk0)
        return [
            remote(x1.at[rows - SHIFT :, span, :], top.at[:, span, :], hsend.at[0, k], hrecv.at[0, k], at(1, 0)),
            remote(x1.at[:SHIFT, span, :], bot.at[:, span, :], hsend.at[1, k], hrecv.at[1, k], at(-1, 0)),
        ]

    def regular(k, _):
        span = pl.ds(pl.multiple_of(k * chunk0, chunk0), chunk0)
        y = first_chunk(x_ref[:, span, :].astype(f32), w, heads, hmask).astype(f32)
        m = WIN * WIN
        y = jnp.concatenate(
            [y[g * m : (g + 1) * m].reshape(WIN, WIN, width) for g in range(chunk0 // WIN)], axis=1
        )
        x1[:, span, :] = y.astype(bf16)
        for c in halo(k):
            c.start()
        return 0

    lax.fori_loop(0, cols // chunk0, regular, 0)
    edge = side.shape[2]
    edges = []
    for s, dc in ((0, 1), (1, -1)):
        span = slice(cols - edge, cols) if dc == 1 else slice(0, edge)
        edges.append(remote(x1.at[:, span, :], side.at[s], esend.at[s, 0], erecv.at[s, 0], at(0, dc)))
        edges.append(
            remote(x1.at[rows - SHIFT :, span, :], corner.at[s, 0], esend.at[s, 1], erecv.at[s, 1], at(1, dc))
        )
        edges.append(remote(x1.at[:SHIFT, span, :], corner.at[s, 1], esend.at[s, 2], erecv.at[s, 2], at(-1, dc)))
    for c in edges:
        c.start()
    settle(1)
    ext[SHIFT : SHIFT + rows, SHIFT : SHIFT + cols, :] = x1[...].astype(f32)
    for k in range(cols // chunk0):
        for c in halo(k):
            c.wait()
    for c in edges:
        c.wait()
    ext[:SHIFT, SHIFT : SHIFT + cols, :] = top[...].astype(f32)
    ext[SHIFT + rows :, SHIFT : SHIFT + cols, :] = bot[...].astype(f32)
    for s in range(2):
        take = slice(edge - SHIFT, edge) if s == 0 else slice(0, SHIFT)
        put = slice(0, SHIFT) if s == 0 else slice(SHIFT + cols, 2 * SHIFT + cols)
        ext[SHIFT : SHIFT + rows, put, :] = side[s].astype(f32)[:, take, :]
        ext[:SHIFT, put, :] = corner[s, 0].astype(f32)[:, take, :]
        ext[SHIFT + rows :, put, :] = corner[s, 1].astype(f32)[:, take, :]
    half = WIN // 2

    def shifted(k, _):
        span = pl.ds(pl.multiple_of(k * chunk1, WIN), chunk1)
        y = second_chunk(ext[:, span, :], regb[:, span, :], w, heads, hmask).astype(f32)
        m = half * WIN
        g = chunk1 // WIN
        for r in range(2):
            for q in range(g):
                e = (r * g + q) * m
                place = pl.ds(pl.multiple_of(k * chunk1 + q * WIN, WIN), WIN)
                res[r * half : (r + 1) * half, place, :] = y[e : e + m].reshape(half, WIN, width)
        return 0

    lax.fori_loop(0, (cols + 2 * SHIFT) // chunk1, shifted, 0)
    o_ref[...] = res[:, SHIFT : SHIFT + cols, :].astype(bf16)
    for c in list(direct.values()) + list(relays.values()):
        c.wait_send()


def chunk_of(windows, most):
    return max(d for d in range(1, most + 1) if windows % d == 0) * WIN


def on_device(*args):
    x, labels, rel_index = args[:3]
    qkv_weight, qkv_bias, bias_table, proj_weight = args[5:9]
    fc1_weight, fc1_bias, fc2_weight = args[10:13]
    rows, cols, width = x.shape
    n = lax.axis_size("ch")
    heads = bias_table.shape[2] * n
    hidden = fc1_weight.shape[2] * n
    chunk0, chunk1 = chunk_of(cols // WIN, 8), chunk_of(cols // WIN + 1, 11)
    tall, wide = rows + 2 * SHIFT, cols + 2 * SHIFT
    edge, keys = 16, WIN * WIN
    dma = pltpu.SemaphoreType.DMA
    vm = pltpu.VMEM
    entries = bias_table.shape[1] + -bias_table.shape[1] % 128
    scratch = [
        vm((tall, wide, width), f32), vm((tall, wide, 128), f32), vm((rows, wide, width), f32),
        vm((rows, cols, width), bf16), vm((SHIFT, cols, width), bf16), vm((SHIFT, cols, width), bf16),
        vm((2, rows, edge, width), bf16), vm((2, 2, SHIFT, edge, width), bf16), vm((8, rows, cols), jnp.int32),
        vm((entries, 128), f32), vm((BLOCKS, 8, entries), f32), vm((n, BLOCKS, 8, entries), f32),
        vm((n,) + qkv_weight.shape, bf16), vm((n,) + qkv_bias.shape, f32), vm((n,) + fc1_bias.shape, f32),
        vm((BLOCKS, width, 3 * width), bf16), vm((BLOCKS, 1, 3 * width), f32),
        vm((BLOCKS, keys, heads * keys), f32), vm((BLOCKS, width, width), bf16),
        vm((BLOCKS, width, hidden), bf16), vm((BLOCKS, 1, hidden), f32), vm((BLOCKS, hidden, width), bf16),
        dma((n - 1, BLOCKS + 1, 4)), dma((n - 1, BLOCKS + 1, 4)),
        dma((n - 1, BLOCKS, 4)), dma((n - 1, BLOCKS, 4)),
        dma((8,)), dma((8,)), dma((2, cols // chunk0)), dma((2, cols // chunk0)), dma((2, 3)), dma((2, 3)),
        dma((7,)),
    ]
    vmem = pl.BlockSpec(memory_space=vm)
    return pl.pallas_call(
        functools.partial(fused, heads, chunk0, chunk1),
        out_shape=jax.ShapeDtypeStruct(x.shape, bf16),
        in_specs=[vmem] * len(args),
        out_specs=vmem,
        scratch_shapes=scratch,
        compiler_params=pltpu.CompilerParams(
            collective_id=0, has_side_effects=True, vmem_limit_bytes=60 * 1024 * 1024
        ),
        name="fused",
    )(*args)


def solution(mesh):
    in_specs = (
        P(("row", "ch"), "col", None), P(("row", "ch"), "col"), P(), P(), P(),
        P(None, None, None, "ch"), P(None, None, "ch"), P(None, None, "ch"), P(None, "ch", None), P(),
        P(None, None, "ch"), P(None, "ch"), P(None, "ch", None), P(),
    )
    out_specs = P(("row", "ch"), "col", None)
    return jax.shard_map(on_device, mesh=mesh, in_specs=in_specs, out_specs=out_specs, check_vma=False)
```

time: 101 us -> 64.7 us (0.64); the launches traced: 99.6 us -> 64.5 us
  blocking collectives: 37 us -> 0 us
  Pallas kernels: 33.9 us -> 58.8 us
  starting transfers between devices: 13.4 us -> 0 us
  matrix products: 4.38 us -> 0 us
  waiting for transfers between devices: 2.37 us -> 0 us
  other arithmetic: 1.45 us -> 0 us
  local copies, waits for them, and re-layouts: 6.94 us -> 5.71 us
    all_gather x7 -> x0, blocking collectives: 37 us -> none  [the longest x1 6.7 us: on_device(): fc2 = lax.all_gather(fc2_weight, 'ch', axis=1, tiled=True)]
    pallas_call x2 -> x1, Pallas kernels: 33.9 us -> 58.8 us  [on_device(): pl.pallas_call(functools.partial(fused, heads, chunk0, chunk1), out_shape...]
    ppermute x8 -> x0, starting transfers between devices: 13.4 us -> none  [the longest x4 11.3 us: padded(): after = lax.ppermute(leading, axis, down)]
    dot_general x2 -> x0, matrix products: 4.38 us -> none  [position_bias(): jnp.dot(onehot, table, precision=lax.Precision.HIGHEST, preferred_element...]
    unnamed x21 -> x6, local copies, waits for them, and re-layouts: 1.49 us -> 5.71 us
    ppermute x8 -> x0, waiting for transfers between devices: 2.37 us -> none  [the longest x4 2.36 us: padded(): before = lax.ppermute(last, axis, up)]
    reshape x6 -> x0, local copies, waits for them, and re-layouts: 1.86 us -> none  [the longest x1 0.82 us: on_device(): qkv.transpose(0, 2, 1, 3).reshape(BLOCKS, width, 3 * width)]
    concatenate x2 -> x0, other arithmetic: 1.32 us -> none  [padded(): shard = jnp.concatenate([before, shard, after], axis=dim)]
  transfers between devices with their start and end apart: 8 -> 0, of which waited for: 2 -> 0; matrix products, arithmetic and copies ran while one was open for 1% -> 0% of each run, Pallas kernels for 0% -> 0%
where the time goes in v1:
time: 64.7 us; the launch traced here: 64.5 us
  Pallas kernels  58.8 us (91%)
  local copies, waits for them, and re-layouts  5.71 us (9%)
    pallas_call x1, Pallas kernels, on_device(): pl.pallas_call(functools.partial(fused, heads, chunk0, chunk1), out_shape...  58.8 us
    unnamed x6, local copies, waits for them, and re-layouts  5.71 us

profile of v1, /device:TPU:0, one launch (start us, length us, event | category | flops | bytes accessed | tf_op | source)
XLA Modules:
  0.0 64.5 jit_solution(12047772524487689554)
XLA Ops:
  0.0 1.3 %copy.16.qkv_b = f32[2,3,64]{2,1,0:T(4,128)} copy(f32[2,3,64]{2,0,1:T(2,128)} %param.20) | data formatting | bytes 3072 | tf_op args[6]
  1.3 0.0 copy-start
  1.3 1.7 %copy.15.qkv_w = bf16[2,3,128,64]{3,2,1,0:T(8,128)(2,1)} copy(bf16[2,3,128,64]{2,3,1,0:T(8,128)(2,1)} %param.19) | data formatting | bytes 196608 | tf_op args[5]
  3.0 0.0 copy-done
  3.0 0.8 %copy.17.table = f32[2,225,2]{2,1,0:T(8,128)} copy(f32[2,225,2]{1,2,0:T(2,128)S(1)} %copy-done) | data formatting | bytes 7200 | tf_op args[7]
  3.8 58.8 %fused.1 = bf16[8,256,128]{2,1,0:T(8,128)(2,1)} custom-call(bf16[8,256,128]{2,1,0:T(8,128)(2,1)} %x_ref.1, s32[8,256]{1,0:T(8,128)} %lab_ref.1, s32[64,64]{1,0:T(8,128)} %rel_ref.1, f32[2,2,128]{2,1,0:T(2,128)} %gain.1, f32[2,2,128]{2,1,0:T(2,128)} %shift.1, bf16[2,3,128,64]{3,2,1,0:T(8,128)(2,1)} %copy.15.qkv_w, f32[2,3,64]{2,1,0:T(4,128)} %copy.16.qkv_b, ...), custom_call_target="tpu_custom_call" | custom-call | tf_op jit(solution)/shard_map/fused/pallas_call | solution.py:395
  62.6 1.9 %copy.19 = bf16[8,256,128]{2,1,0:T(8,128)(2,1)} copy(bf16[8,256,128]{2,1,0:T(8,128)(2,1)} %fused.1) | data formatting | bytes 1048576
Async XLA Ops:
  1.3 1.7 %copy-start = (f32[2,225,2]{1,2,0:T(2,128)S(1)}, f32[2,225,2]{1,2,0:T(2,128)}, u32[]{:S(2)}) copy-start(f32[2,225,2]{1,2,0:T(2,128)} %param.21) | copy-start | bytes 10804

commit v2 on v1

--- a/solution.py
+++ b/solution.py
@@ -12,6 +12,8 @@
 BLOCKS = 2
 EPS = 1e-05
 FAR = -1e30
+LOG2E = 1.4426950408889634
+GROUP = 4
 bf16 = jnp.bfloat16
 f32 = jnp.float32
 
@@ -34,30 +36,33 @@
     return x.reshape(x.shape[0] * x.shape[1], x.shape[2])
 
 
-def attend(q, k, v, hmask, bias, heads, depth, far=None):
-    keys = k.shape[0]
-    kb = jnp.concatenate([k] * heads, axis=0) * hmask
-    vb = jnp.concatenate([v] * heads, axis=0) * hmask
-    if far is not None:
-        fq, fk = far
-        q = jnp.concatenate([q, fq], axis=1)
-        kb = jnp.concatenate([kb, jnp.concatenate([fk] * heads, axis=0)], axis=1)
-    s = dot_t(q, kb) * (depth ** (-0.5)) + bias
+def attend(group, hmask, bias, heads, depth):
+    keys, width = group[0][1].shape
     per = 128 // keys
-    parts = []
-    lane = lax.broadcasted_iota(jnp.int32, (s.shape[0], 128), 1)
-    for c in range(0, s.shape[1], 128):
-        t = s[:, c : c + 128]
-        top = None
-        for j in range(per):
-            inside = (lane >= j * keys) & (lane < (j + 1) * keys)
-            peak = jnp.max(jnp.where(inside, t, -jnp.inf), axis=-1, keepdims=True)
-            top = peak if top is None else jnp.where(lane >= j * keys, peak, top)
-        parts.append(jnp.exp(t - top))
-    p = jnp.concatenate(parts, axis=1).astype(bf16)
-    o = dot(p, jnp.concatenate([vb, hmask], axis=1))
-    width = q.shape[1] if far is None else k.shape[1]
-    return (o[:, :width] / o[:, width:]).astype(bf16)
+    scores, values = [], []
+    for q, k, v, far in group:
+        kb = jnp.concatenate([k] * heads, axis=0) * hmask
+        if far is not None:
+            q = jnp.concatenate([q, far[0]], axis=1)
+            kb = jnp.concatenate([kb, jnp.concatenate([far[1]] * heads, axis=0)], axis=1)
+        scores.append(dot_t(q, kb))
+        values.append(jnp.concatenate([jnp.concatenate([v] * heads, axis=0) * hmask, hmask], axis=1))
+    lane = lax.broadcasted_iota(jnp.int32, (scores[0].shape[0], 128), 1)
+    weights = []
+    for s in scores:
+        s = s * (depth ** (-0.5) * LOG2E) + bias
+        parts = []
+        for c in range(0, s.shape[1], 128):
+            t = s[:, c : c + 128]
+            top = None
+            for j in range(per):
+                inside = (lane >= j * keys) & (lane < (j + 1) * keys)
+                peak = jnp.max(jnp.where(inside, t, -jnp.inf), axis=-1, keepdims=True)
+                top = peak if top is None else jnp.where(lane >= j * keys, peak, top)
+            parts.append(jnp.exp2(t - top))
+        weights.append(jnp.concatenate(parts, axis=1).astype(bf16))
+    outs = [dot(p, v) for p, v in zip(weights, values)]
+    return [(o[:, :width] / o[:, width:]).astype(bf16) for o in outs]
 
 
 def finish(x, attended, w, b):
@@ -79,7 +84,7 @@
 
 def qkv_of(x, w, b):
     normed = layer_norm(x, w["gain"][b][0:1], w["shift"][b][0:1])
-    return dot(normed, w["qkv"][b]) + w["qkv_b"][b]
+    return dot_t(normed, rows_of(w["qkv"][b])) + w["qkv_b"][b]
 
 
 def first_chunk(x, w, heads, hmask):
@@ -91,11 +96,12 @@
     triple = qkv_of(toks, w, 0)
     outs = []
     n = WIN * WIN
+    windows = []
     for g in range(wide // WIN):
         t = triple[g * n : (g + 1) * n].astype(bf16)
-        outs.append(
-            attend(t[:, :width], t[:, width : 2 * width], t[:, 2 * width :], hmask, w["bias"][0], heads, depth)
-        )
+        windows.append((t[:, :width], t[:, width : 2 * width], t[:, 2 * width :], None))
+    for g in range(0, len(windows), GROUP):
+        outs += attend(windows[g : g + GROUP], hmask, w["bias"][0], heads, depth)
     return finish(toks, jnp.concatenate(outs, axis=0), w, 0)
 
 
@@ -112,15 +118,14 @@
         triple = qkv_of(jnp.concatenate(xs, axis=0), w, 1)
         own = slice(half * WIN, n) if r == 0 else slice(0, half * WIN)
         bias = w["bias"][1][own, :]
+        windows = []
         for g in range(wide // WIN):
             t = triple[g * n : (g + 1) * n].astype(bf16)
-            outs.append(
-                attend(
-                    t[own, :width], t[:, width : 2 * width], t[:, 2 * width :], hmask, bias, heads, depth,
-                    ((same[g][own] * FAR).astype(bf16), (1.0 - same[g]).astype(bf16)),
-                )
-            )
+            far = (same[g][own] * FAR).astype(bf16), (1.0 - same[g]).astype(bf16)
+            windows.append((t[own, :width], t[:, width : 2 * width], t[:, 2 * width :], far))
             toks.append(xs[g][own])
+        for g in range(0, len(windows), GROUP):
+            outs += attend(windows[g : g + GROUP], hmask, bias, heads, depth)
     return finish(jnp.concatenate(toks, axis=0), jnp.concatenate(outs, axis=0), w, 1)
 
 
@@ -128,8 +133,8 @@
     heads, chunk0, chunk1,
     x_ref, lab_ref, rel_ref, gain, shift, qkv_w, qkv_b, table, proj_w, proj_b, fc1_w, fc1_b, fc2_w, fc2_b,
     o_ref,
-    ext, regb, res, x1, top, bot, side, corner, lab, tsc, tab_own, tab_all,
-    qkv_all, qb_all, f1b_all, qkv, qb, bias, proj, fc1, f1b, fc2,
+    ext, regb, res, x1, top, bot, side, corner, lab, tab_own, tab_all,
+    qb_all, f1b_all, qkv, qb, bias, proj, fc1, f1b, fc2,
     wsend, wrecv, rsend, rrecv, lsend, lrecv, hsend, hrecv, esend, erecv, own_sem,
 ):
     rows, cols, width = x_ref.shape
@@ -159,19 +164,18 @@
             src_ref=src, dst_ref=dst, send_sem=ssem, recv_sem=rsem, device_id=to, device_id_type=mesh_id
         )
 
-    for b in range(BLOCKS):
-        tsc[...] = jnp.zeros_like(tsc)
-        tsc[: table.shape[1], : table.shape[2]] = table[b]
-        tab_own[b] = tsc[...].T[:8]
+    tab_own[...] = jnp.zeros_like(tab_own)
+    tab_own[:, : table.shape[1], : table.shape[2]] = table[...]
     pl.semaphore_wait(barrier, len(targets))
 
-    kh, ph, fh, gh = width // 2, proj_w.shape[1] // 2, width // 2, fc2_w.shape[1] // 2
+    part = width // n
+    kh, ph, fh, gh = qkv_w.shape[2] // 2, proj_w.shape[1] // 2, width // 2, fc2_w.shape[1] // 2
     pw, fw, gw = proj_w.shape[1], fc1_w.shape[2], fc2_w.shape[1]
 
     def pieces(b, owner):
         k0, p0, f0, g0 = (pl.multiple_of(core * v, 16) for v in (kh, ph, fh, gh))
         return [
-            (qkv_w.at[b, :, pl.ds(k0, kh), :], qkv_all.at[owner, b, :, pl.ds(k0, kh), :]),
+            (qkv_w.at[b, :, pl.ds(k0, kh), :], qkv.at[b, :, pl.ds(pl.multiple_of(owner * part + k0, 16), kh), :]),
             (proj_w.at[b, pl.ds(p0, ph), :], proj.at[b, pl.ds(pl.multiple_of(owner * pw + p0, 16), ph), :]),
             (
                 fc1_w.at[b, pl.ds(f0, fh), :],
@@ -194,16 +198,18 @@
             smalls.append(remote(src, dst, wsend.at[d - 1, BLOCKS, i], wrecv.at[d - 1, BLOCKS, i], to))
     for c in smalls:
         c.start()
-    for b in range(BLOCKS):
-        for d in range(1, n):
-            for i in range(4):
-                direct[d, b, i].start()
+    for d in range(1, n):
+        for i in range(4):
+            direct[d, 0, i].start()
     labels = []
     for i, d in enumerate(around):
         labels.append(remote(lab_ref, lab.at[i], lsend.at[i], lrecv.at[i], at(-d[0], -d[1])))
         labels[-1].start()
+    for d in range(1, n):
+        for i in range(4):
+            direct[d, 1, i].start()
     locals_ = [
-        (qkv_w, qkv_all.at[ch]),
+        (qkv_w, qkv.at[:, :, pl.ds(pl.multiple_of(ch * part, 16), part), :]),
         (proj_w, proj.at[:, pl.ds(pl.multiple_of(ch * pw, 16), pw), :]),
         (fc1_w, fc1.at[:, :, pl.ds(pl.multiple_of(ch * fw, 128), fw)]),
         (fc2_w, fc2.at[:, pl.ds(pl.multiple_of(ch * gw, 16), gw), :]),
@@ -217,14 +223,13 @@
     for c in smalls:
         c.wait()
 
-    part = width // n
     keys = WIN * WIN
     for j in range(n):
         for b in range(BLOCKS):
             for m in range(3):
-                qb[b, :, m * width + j * part : m * width + (j + 1) * part] = qb_all[j, b, m : m + 1, :]
+                qb[b, :, m * width + j * part : m * width + (j + 1) * part] = qb_all[j, m, b : b + 1, :]
             f1b[b, :, j * fw : (j + 1) * fw] = f1b_all[j, b : b + 1, :]
-    local_heads = table.shape[2]
+    local_heads = table.shape[1]
     per = 128 // keys
     idx = jnp.concatenate([rel_ref[...]] * per, axis=1)
     lane = lax.broadcasted_iota(jnp.int32, idx.shape, 1)
@@ -240,7 +245,7 @@
                     here = jnp.take_along_axis(piece, idx & 127, axis=1, mode="promise_in_bounds")
                     got = here if got is None else jnp.where(idx >= c, here, got)
                 out = got if out is None else jnp.where(lane >= j * keys, got, out)
-            bias[b, :, t * 128 : (t + 1) * 128] = out
+            bias[b, :, t * 128 : (t + 1) * 128] = out * LOG2E
 
     def bring(b):
         for d in range(1, n):
@@ -252,10 +257,49 @@
         for d in range(1, n):
             for i in range(4):
                 relays[d, b, i].wait_recv()
-        for j in range(n):
-            for m in range(3):
-                qkv[b, :, m * width + j * part : m * width + (j + 1) * part] = qkv_all[j, b, m]
-
+
+    bring(0)
+    settle(0)
+    w = {
+        "gain": gain, "shift": shift, "qkv": qkv, "qkv_b": qb, "bias": bias, "proj": proj,
+        "proj_b": [proj_b[b : b + 1] for b in range(BLOCKS)], "fc1": fc1, "fc1_b": f1b, "fc2": fc2,
+        "fc2_b": [fc2_b[b : b + 1] for b in range(BLOCKS)],
+    }
+    hmask = head_mask(heads, keys, width)
+
+    def halo(k):
+        span = pl.ds(pl.multiple_of(k * chunk0, chunk0), chunk0)
+        return [
+            remote(x1.at[rows - SHIFT :, span, :], top.at[:, span, :], hsend.at[0, k], hrecv.at[0, k], at(1, 0)),
+            remote(x1.at[:SHIFT, span, :], bot.at[:, span, :], hsend.at[1, k], hrecv.at[1, k], at(-1, 0)),
+        ]
+
+    def regular(step, _):
+        k = lax.rem(step + 1, cols // chunk0)
+        span = pl.ds(pl.multiple_of(k * chunk0, chunk0), chunk0)
+        y = first_chunk(x_ref[:, span, :].astype(f32), w, heads, hmask).astype(f32)
+        m = WIN * WIN
+        y = jnp.concatenate(
+            [y[g * m : (g + 1) * m].reshape(WIN, WIN, width) for g in range(chunk0 // WIN)], axis=1
+        )
+        x1[:, span, :] = y.astype(bf16)
+        for c in halo(k):
+            c.start()
+        return 0
+
+    lax.fori_loop(0, cols // chunk0, regular, 0)
+    edge = side.shape[2]
+    edges = []
+    for s, dc in ((0, 1), (1, -1)):
+        span = slice(cols - edge, cols) if dc == 1 else slice(0, edge)
+        edges.append(remote(x1.at[:, span, :], side.at[s], esend.at[s, 0], erecv.at[s, 0], at(0, dc)))
+        edges.append(
+            remote(x1.at[rows - SHIFT :, span, :], corner.at[s, 0], esend.at[s, 1], erecv.at[s, 1], at(1, dc))
+        )
+        edges.append(remote(x1.at[:SHIFT, span, :], corner.at[s, 1], esend.at[s, 2], erecv.at[s, 2], at(-1, dc)))
+    for c in edges:
+        c.start()
+    bring(1)
     for c in labels:
         c.wait()
     def column(up, mid, down):
@@ -281,64 +325,16 @@
     pick = lax.broadcasted_iota(jnp.int32, (tall, 128), 0)
     for r in range(tall):
         regb[r] = dot(turned, (pick == r).astype(f32).astype(bf16))
-
-    bring(0)
-    bring(1)
-    settle(0)
-
-    w = {
-        "gain": gain, "shift": shift, "qkv": qkv, "qkv_b": qb, "bias": bias, "proj": proj,
-        "proj_b": [proj_b[b : b + 1] for b in range(BLOCKS)], "fc1": fc1, "fc1_b": f1b, "fc2": fc2,
-        "fc2_b": [fc2_b[b : b + 1] for b in range(BLOCKS)],
-    }
-    hmask = head_mask(heads, keys, width)
-
-    def halo(k):
-        span = pl.ds(pl.multiple_of(k * chunk0, chunk0), chunk0)
-        return [
-            remote(x1.at[rows - SHIFT :, span, :], top.at[:, span, :], hsend.at[0, k], hrecv.at[0, k], at(1, 0)),
-            remote(x1.at[:SHIFT, span, :], bot.at[:, span, :], hsend.at[1, k], hrecv.at[1, k], at(-1, 0)),
-        ]
-
-    def regular(k, _):
-        span = pl.ds(pl.multiple_of(k * chunk0, chunk0), chunk0)
-        y = first_chunk(x_ref[:, span, :].astype(f32), w, heads, hmask).astype(f32)
-        m = WIN * WIN
-        y = jnp.concatenate(
-            [y[g * m : (g + 1) * m].reshape(WIN, WIN, width) for g in range(chunk0 // WIN)], axis=1
-        )
-        x1[:, span, :] = y.astype(bf16)
-        for c in halo(k):
-            c.start()
-        return 0
-
-    lax.fori_loop(0, cols // chunk0, regular, 0)
-    edge = side.shape[2]
-    edges = []
-    for s, dc in ((0, 1), (1, -1)):
-        span = slice(cols - edge, cols) if dc == 1 else slice(0, edge)
-        edges.append(remote(x1.at[:, span, :], side.at[s], esend.at[s, 0], erecv.at[s, 0], at(0, dc)))
-        edges.append(
-            remote(x1.at[rows - SHIFT :, span, :], corner.at[s, 0], esend.at[s, 1], erecv.at[s, 1], at(1, dc))
-        )
-        edges.append(remote(x1.at[:SHIFT, span, :], corner.at[s, 1], esend.at[s, 2], erecv.at[s, 2], at(-1, dc)))
-    for c in edges:
-        c.start()
     settle(1)
     ext[SHIFT : SHIFT + rows, SHIFT : SHIFT + cols, :] = x1[...].astype(f32)
-    for k in range(cols // chunk0):
+    def land(k):
+        span = slice(k * chunk0, (k + 1) * chunk0)
+        put = slice(SHIFT + k * chunk0, SHIFT + (k + 1) * chunk0)
         for c in halo(k):
             c.wait()
-    for c in edges:
-        c.wait()
-    ext[:SHIFT, SHIFT : SHIFT + cols, :] = top[...].astype(f32)
-    ext[SHIFT + rows :, SHIFT : SHIFT + cols, :] = bot[...].astype(f32)
-    for s in range(2):
-        take = slice(edge - SHIFT, edge) if s == 0 else slice(0, SHIFT)
-        put = slice(0, SHIFT) if s == 0 else slice(SHIFT + cols, 2 * SHIFT + cols)
-        ext[SHIFT : SHIFT + rows, put, :] = side[s].astype(f32)[:, take, :]
-        ext[:SHIFT, put, :] = corner[s, 0].astype(f32)[:, take, :]
-        ext[SHIFT + rows :, put, :] = corner[s, 1].astype(f32)[:, take, :]
+        ext[:SHIFT, put, :] = top[:, span, :].astype(f32)
+        ext[SHIFT + rows :, put, :] = bot[:, span, :].astype(f32)
+
     half = WIN // 2
 
     def shifted(k, _):
@@ -353,7 +349,28 @@
                 res[r * half : (r + 1) * half, place, :] = y[e : e + m].reshape(half, WIN, width)
         return 0
 
-    lax.fori_loop(0, (cols + 2 * SHIFT) // chunk1, shifted, 0)
+    steps = (cols + 2 * SHIFT) // chunk1
+    first, last = (chunk1 - SHIFT) // chunk0, ((steps - 1) * chunk1 - SHIFT - 1) // chunk0
+    ready = range(first, last + 1) if steps > 2 else ()
+    for k in ready:
+        land(k)
+    if steps > 2:
+        lax.fori_loop(1, steps - 1, shifted, 0)
+    for k in range(cols // chunk0):
+        if k not in ready:
+            land(k)
+    for c in edges:
+        c.wait()
+    for s in range(2):
+        take = slice(edge - SHIFT, edge) if s == 0 else slice(0, SHIFT)
+        put = slice(0, SHIFT) if s == 0 else slice(SHIFT + cols, 2 * SHIFT + cols)
+        ext[SHIFT : SHIFT + rows, put, :] = side[s].astype(f32)[:, take, :]
+        ext[:SHIFT, put, :] = corner[s, 0].astype(f32)[:, take, :]
+        ext[SHIFT + rows :, put, :] = corner[s, 1].astype(f32)[:, take, :]
+    if steps > 1:
+        lax.fori_loop(0, 2, lambda i, c: shifted(i * (steps - 1), c), 0)
+    else:
+        shifted(0, 0)
     o_ref[...] = res[:, SHIFT : SHIFT + cols, :].astype(bf16)
     for c in list(direct.values()) + list(relays.values()):
         c.wait_send()
@@ -370,6 +387,10 @@
     rows, cols, width = x.shape
     n = lax.axis_size("ch")
     heads = bias_table.shape[2] * n
+    args = list(args)
+    args[5] = qkv_weight.swapaxes(2, 3)
+    args[6] = qkv_bias.swapaxes(0, 1)
+    args[7] = bias_table.swapaxes(1, 2)
     hidden = fc1_weight.shape[2] * n
     chunk0, chunk1 = chunk_of(cols // WIN, 8), chunk_of(cols // WIN + 1, 11)
     tall, wide = rows + 2 * SHIFT, cols + 2 * SHIFT
@@ -381,9 +402,9 @@
         vm((tall, wide, width), f32), vm((tall, wide, 128), f32), vm((rows, wide, width), f32),
         vm((rows, cols, width), bf16), vm((SHIFT, cols, width), bf16), vm((SHIFT, cols, width), bf16),
         vm((2, rows, edge, width), bf16), vm((2, 2, SHIFT, edge, width), bf16), vm((8, rows, cols), jnp.int32),
-        vm((entries, 128), f32), vm((BLOCKS, 8, entries), f32), vm((n, BLOCKS, 8, entries), f32),
-        vm((n,) + qkv_weight.shape, bf16), vm((n,) + qkv_bias.shape, f32), vm((n,) + fc1_bias.shape, f32),
-        vm((BLOCKS, width, 3 * width), bf16), vm((BLOCKS, 1, 3 * width), f32),
+        vm((BLOCKS, 8, entries), f32), vm((n, BLOCKS, 8, entries), f32),
+        vm((n,) + args[6].shape, f32), vm((n,) + fc1_bias.shape, f32),
+        vm((BLOCKS, 3, width, width), bf16), vm((BLOCKS, 1, 3 * width), f32),
         vm((BLOCKS, keys, heads * keys), f32), vm((BLOCKS, width, width), bf16),
         vm((BLOCKS, width, hidden), bf16), vm((BLOCKS, 1, hidden), f32), vm((BLOCKS, hidden, width), bf16),
         dma((n - 1, BLOCKS + 1, 4)), dma((n - 1, BLOCKS + 1, 4)),

time: 64.7 us -> 43 us (0.66)
  Pallas kernels: 58.8 us -> 41 us
  local copies, waits for them, and re-layouts: 5.71 us -> 1.87 us
    pallas_call x1, Pallas kernels: 58.8 us -> 41 us  [on_device(): pl.pallas_call(functools.partial(fused, heads, chunk0, chunk1), out_shape...]
    unnamed x6 -> x1, local copies, waits for them, and re-layouts: 5.71 us -> 1.87 us
where the time goes in v2:
time: 43 us; the launch traced here: 42.9 us
  Pallas kernels  41 us (95%)
  local copies, waits for them, and re-layouts  1.87 us (4%)
    pallas_call x1, Pallas kernels, on_device(): pl.pallas_call(functools.partial(fused, heads, chunk0, chunk1), out_shape...  41 us
    unnamed x1, local copies, waits for them, and re-layouts  1.87 us

profile of v2, /device:TPU:0, one launch (start us, length us, event | category | flops | bytes accessed | tf_op | source)
XLA Modules:
  0.0 42.9 jit_solution(9697425754901421188)
XLA Ops:
  0.0 41.0 %fused.1 = bf16[8,256,128]{2,1,0:T(8,128)(2,1)} custom-call(bf16[8,256,128]{2,1,0:T(8,128)(2,1)} %x_ref.1, s32[8,256]{1,0:T(8,128)} %lab_ref.1, s32[64,64]{1,0:T(8,128)} %rel_ref.1, f32[2,2,128]{2,1,0:T(2,128)} %gain.1, f32[2,2,128]{2,1,0:T(2,128)} %shift.1, bf16[2,3,64,128]{3,2,1,0:T(8,128)(2,1)} %bitcast.3, f32[3,2,64]{2,1,0:T(2,128)} %bitcast.5, ...), custom_call_target="tpu_custom_call" | custom-call | tf_op jit(solution)/shard_map/fused/pallas_call | solution.py:416
  41.0 1.9 %copy.16 = bf16[8,256,128]{2,1,0:T(8,128)(2,1)} copy(bf16[8,256,128]{2,1,0:T(8,128)(2,1)} %fused.1) | data formatting | bytes 1048576

commit v3 on v2

--- a/solution.py
+++ b/solution.py
@@ -13,7 +13,7 @@
 EPS = 1e-05
 FAR = -1e30
 LOG2E = 1.4426950408889634
-GROUP = 4
+GROUP = 22
 bf16 = jnp.bfloat16
 f32 = jnp.float32
 
@@ -36,11 +36,11 @@
     return x.reshape(x.shape[0] * x.shape[1], x.shape[2])
 
 
-def attend(group, hmask, bias, heads, depth):
+def attend(group, hmask, heads, depth):
     keys, width = group[0][1].shape
     per = 128 // keys
     scores, values = [], []
-    for q, k, v, far in group:
+    for q, k, v, far, _ in group:
         kb = jnp.concatenate([k] * heads, axis=0) * hmask
         if far is not None:
             q = jnp.concatenate([q, far[0]], axis=1)
@@ -49,7 +49,7 @@
         values.append(jnp.concatenate([jnp.concatenate([v] * heads, axis=0) * hmask, hmask], axis=1))
     lane = lax.broadcasted_iota(jnp.int32, (scores[0].shape[0], 128), 1)
     weights = []
-    for s in scores:
+    for s, (_, _, _, _, bias) in zip(scores, group):
         s = s * (depth ** (-0.5) * LOG2E) + bias
         parts = []
         for c in range(0, s.shape[1], 128):
@@ -99,9 +99,9 @@
     windows = []
     for g in range(wide // WIN):
         t = triple[g * n : (g + 1) * n].astype(bf16)
-        windows.append((t[:, :width], t[:, width : 2 * width], t[:, 2 * width :], None))
+        windows.append((t[:, :width], t[:, width : 2 * width], t[:, 2 * width :], None, w["bias"][0]))
     for g in range(0, len(windows), GROUP):
-        outs += attend(windows[g : g + GROUP], hmask, w["bias"][0], heads, depth)
+        outs += attend(windows[g : g + GROUP], hmask, heads, depth)
     return finish(toks, jnp.concatenate(outs, axis=0), w, 0)
 
 
@@ -110,7 +110,7 @@
     rows, wide, width = x.shape
     depth = width // heads
     half = WIN // 2
-    outs, toks = [], []
+    outs, toks, windows = [], [], []
     n = WIN * WIN
     for r in range(0, rows, WIN):
         xs = [rows_of(x[r : r + WIN, c : c + WIN]) for c in range(0, wide, WIN)]
@@ -118,14 +118,13 @@
         triple = qkv_of(jnp.concatenate(xs, axis=0), w, 1)
         own = slice(half * WIN, n) if r == 0 else slice(0, half * WIN)
         bias = w["bias"][1][own, :]
-        windows = []
         for g in range(wide // WIN):
             t = triple[g * n : (g + 1) * n].astype(bf16)
             far = (same[g][own] * FAR).astype(bf16), (1.0 - same[g]).astype(bf16)
-            windows.append((t[own, :width], t[:, width : 2 * width], t[:, 2 * width :], far))
+            windows.append((t[own, :width], t[:, width : 2 * width], t[:, 2 * width :], far, bias))
             toks.append(xs[g][own])
-        for g in range(0, len(windows), GROUP):
-            outs += attend(windows[g : g + GROUP], hmask, bias, heads, depth)
+    for g in range(0, len(windows), GROUP):
+        outs += attend(windows[g : g + GROUP], hmask, heads, depth)
     return finish(jnp.concatenate(toks, axis=0), jnp.concatenate(outs, axis=0), w, 1)
 
 
@@ -392,7 +391,7 @@
     args[6] = qkv_bias.swapaxes(0, 1)
     args[7] = bias_table.swapaxes(1, 2)
     hidden = fc1_weight.shape[2] * n
-    chunk0, chunk1 = chunk_of(cols // WIN, 8), chunk_of(cols // WIN + 1, 11)
+    chunk0, chunk1 = chunk_of(cols // WIN, 4), chunk_of(cols // WIN + 1, 11)
     tall, wide = rows + 2 * SHIFT, cols + 2 * SHIFT
     edge, keys = 16, WIN * WIN
     dma = pltpu.SemaphoreType.DMA

time: 43 us -> 39.7 us (0.923)
  Pallas kernels: 41 us -> 37.6 us
    pallas_call x1, Pallas kernels: 41 us -> 37.6 us  [on_device(): pl.pallas_call(functools.partial(fused, heads, chunk0, chunk1), out_shape...]
where the time goes in v3:
time: 39.7 us; the launch traced here: 39.5 us
  Pallas kernels  37.6 us (95%)
  local copies, waits for them, and re-layouts  1.87 us (5%)
    pallas_call x1, Pallas kernels, on_device(): pl.pallas_call(functools.partial(fused, heads, chunk0, chunk1), out_shape...  37.6 us
    unnamed x1, local copies, waits for them, and re-layouts  1.87 us

profile of v3, /device:TPU:0, one launch (start us, length us, event | category | flops | bytes accessed | tf_op | source)
XLA Modules:
  0.0 39.5 jit_solution(12628997326332243945)
XLA Ops:
  0.0 37.6 %fused.1 = bf16[8,256,128]{2,1,0:T(8,128)(2,1)} custom-call(bf16[8,256,128]{2,1,0:T(8,128)(2,1)} %x_ref.1, s32[8,256]{1,0:T(8,128)} %lab_ref.1, s32[64,64]{1,0:T(8,128)} %rel_ref.1, f32[2,2,128]{2,1,0:T(2,128)} %gain.1, f32[2,2,128]{2,1,0:T(2,128)} %shift.1, bf16[2,3,64,128]{3,2,1,0:T(8,128)(2,1)} %bitcast.3, f32[3,2,64]{2,1,0:T(2,128)} %bitcast.5, ...), custom_call_target="tpu_custom_call" | custom-call | tf_op jit(solution)/shard_map/fused/pallas_call | solution.py:415
  37.6 1.9 %copy.16 = bf16[8,256,128]{2,1,0:T(8,128)(2,1)} copy(bf16[8,256,128]{2,1,0:T(8,128)(2,1)} %fused.1) | data formatting | bytes 1048576
